TPU v7x, 256 devices: a whole 4x4x8 slice. The times are simulated.
256 devices in a mesh: blk: 8 (over x, core), grp: 32 (over z, y).
Axes of the slice: x: 4, y: 4, z: 8, core: 2. Of those that a mesh axis runs over, the one named last changes fastest.
Arguments:
- features: float32 [393216, 256], P(('blk', 'grp')), may hold values from -6 to 6
- initial: bfloat16 [393216, 256], P(('blk', 'grp')), may hold values from -6 to 6
- history: bfloat16 [393216, 256], P(('blk', 'grp')), may hold values from -6 to 6
- weight: bfloat16 [256, 256], replicated, may hold values from -0.375 to 0.375
- column_ids: int32 [3072, 16], P(('blk', 'grp')), may hold values from 0 to 51, as said below
- block_values: bfloat16 [3072, 16, 128, 128], P(('blk', 'grp')), may hold values from -0.125 to 0.125
- group_table: int32 [8, 32, 32], P('blk'), may hold values from 0 to 11
- loop_table: int32 [32, 8, 8], P('grp'), may hold values from 0 to 11
Outputs:
- refreshed: float32 [393216, 256], P(('blk', 'grp'))
- inbox: float32 [393216, 256], P(('blk', 'grp'))
Inputs may be any that keep to these rules, and one draw needn't show every extreme that they name: `column_ids`: among the 16 entries of the 12 row tiles of one device, every slot from 0 to 12 + 32 + 8 - 1 appears at least once.
All inputs are finite; a program needn't handle non-finite values.
Results may differ from a plain program's by a relative error of at most 0.004.
Values may be sent and summed in bfloat16 or wider, within the bound.
A program may use at most 128 MiB of HBM per device.

v0:
```python
import jax
import jax.numpy as jnp
from jax import lax
from jax.sharding import PartitionSpec as P

teleport = 0.1
mapping_share = 0.5


def body(features, initial, history, weight, column_ids, block_values, group_table, loop_table):
    group_count = lax.axis_size("grp")
    group_pos = lax.axis_index("grp")
    loop_pos = lax.axis_index("blk")
    tiles, entries = column_ids.shape
    edge = block_values.shape[2]
    hidden = features.shape[1]
    stale = history.reshape(tiles, edge, hidden)
    group_rows = group_table[0]
    loop_rows = loop_table[0]
    serve_group = lax.dynamic_index_in_dim(group_rows, group_pos, 0, keepdims=False)
    serve_loop = lax.dynamic_index_in_dim(loop_rows, loop_pos, 0, keepdims=False)
    own_blocks = features.astype(jnp.bfloat16).reshape(tiles, edge, hidden)
    from_group = lax.all_to_all(stale[serve_group], "grp", split_axis=0, concat_axis=0, tiled=True)
    from_loop = lax.all_to_all(stale[serve_loop], "blk", split_axis=0, concat_axis=0, tiled=True)
    sources = jnp.concatenate([own_blocks, from_group, from_loop], axis=0)
    slots = sources.shape[0]
    picked = sources[column_ids]
    gathered = jnp.einsum(
        "tkij,tkjh->tih", block_values, picked, preferred_element_type=jnp.float32
    )
    start = initial.reshape(tiles, edge, hidden).astype(jnp.float32)
    mixed = (
        ((1.0 - teleport) * gathered + teleport * start)
        .astype(jnp.bfloat16)
        .reshape(tiles * edge, hidden)
    )
    product = jnp.dot(mixed, weight, preferred_element_type=jnp.float32)
    refreshed = jax.nn.relu(
        (1.0 - mapping_share) * mixed.astype(jnp.float32) + mapping_share * product
    )
    outgoing = refreshed.astype(jnp.bfloat16).reshape(tiles, edge, hidden)
    each = jnp.einsum("tkij,tih->tkjh", block_values, outgoing, preferred_element_type=jnp.float32)
    selector = (column_ids[:, :, None] == jnp.arange(slots)[None, None, :]).astype(jnp.float32)
    messages = jnp.einsum("tks,tkjh->sjh", selector, each, precision=lax.Precision.HIGHEST).astype(
        jnp.bfloat16
    )
    incoming_group = lax.all_to_all(
        messages[tiles : tiles + group_count], "grp", split_axis=0, concat_axis=0, tiled=True
    )
    incoming_loop = lax.all_to_all(
        messages[tiles + group_count :], "blk", split_axis=0, concat_axis=0, tiled=True
    )
    block_range = jnp.arange(tiles)
    group_hit = (serve_group[:, None] == block_range[None, :]).astype(jnp.bfloat16)
    loop_hit = (serve_loop[:, None] == block_range[None, :]).astype(jnp.bfloat16)
    inbox = jnp.einsum("gl,gjh->ljh", group_hit, incoming_group, preferred_element_type=jnp.float32)
    inbox = inbox + jnp.einsum(
        "gl,gjh->ljh", loop_hit, incoming_loop, preferred_element_type=jnp.float32
    )
    return (refreshed, inbox.reshape(tiles * edge, hidden))


def solution(mesh):
    in_specs = (
        P(("blk", "grp"), None),
        P(("blk", "grp"), None),
        P(("blk", "grp"), None),
        P(),
        P(("blk", "grp"), None),
        P(("blk", "grp"), None, None, None),
        P("blk", None, None),
        P("grp", None, None),
    )
    out_specs = (P(("blk", "grp"), None), P(("blk", "grp"), None))
    return jax.shard_map(body, mesh=mesh, in_specs=in_specs, out_specs=out_specs, check_vma=False)
```

profile of v0, /device:TPU:1, one launch (start us, length us, event | category | flops | bytes accessed | tf_op | source)
XLA Modules:
  0.0 209.2 jit_solution(15727803676338859610)
XLA Ops:
  0.7 0.8 fusion.24
  1.8 1.4 gather_fusion.1
  3.2 6.6 %all-to-all-start.1 = ((bf16[8,128,256]{2,1,0:T(8,128)(2,1)}), bf16[8,128,256]{2,1,0:T(8,128)(2,1)S(1)}, u32[]{:S(2)}, u32[]{:S(2)}) async-start(bf16[8,128,256]{2,1,0:T(8,128)(2,1)} %gather_fusion.1), calls=%async_computation.1 | async-start | bytes 1048576 | tf_op jit(solution)/shard_map/all_to_all | solution.py:24
  9.8 0.7 fusion.23
  10.5 2.0 gather_fusion
  12.5 6.7 %all-to-all-done.1 = bf16[8,128,256]{2,1,0:T(8,128)(2,1)S(1)} async-done(((bf16[8,128,256]{2,1,0:T(8,128)(2,1)}), bf16[8,128,256]{2,1,0:T(8,128)(2,1)S(1)}, u32[]{:S(2)}, u32[]{:S(2)}) %all-to-all-start.1) | async-done | bytes 524320 | tf_op jit(solution)/shard_map/all_to_all | solution.py:24
  19.1 0.8 copy-done.3
  19.9 10.4 %all-to-all-start = ((bf16[32,128,256]{2,1,0:T(8,128)(2,1)}), bf16[32,128,256]{2,1,0:T(8,128)(2,1)S(1)}, u32[]{:S(2)}, u32[]{:S(2)}) async-start(bf16[32,128,256]{2,1,0:T(8,128)(2,1)} %gather_fusion), calls=%async_computation | async-start | bytes 4194304 | tf_op jit(solution)/shard_map/all_to_all | solution.py:23
  30.4 2.4 %convert_element_type.22 = bf16[1536,256]{1,0:T(8,128)(2,1)} convert(f32[1536,256]{1,0:T(8,128)} %param.8) | non-fusion elementwise | flops 393216 | bytes 2359296 | tf_op jit(solution)/shard_map/convert_element_type | solution.py:22
  32.8 9.2 %copy.11 = bf16[12,16,128,128]{2,1,0,3:T(8,128)(2,1)} copy(bf16[12,16,128,128]{3,2,1,0:T(8,128)(2,1)} %param.13) | data formatting | bytes 12582912 | tf_op args[5]
  42.0 1.3 convert_multiply_fusion
  43.3 35.3 %all-to-all-done = bf16[32,128,256]{2,1,0:T(8,128)(2,1)S(1)} async-done(((bf16[32,128,256]{2,1,0:T(8,128)(2,1)}), bf16[32,128,256]{2,1,0:T(8,128)(2,1)S(1)}, u32[]{:S(2)}, u32[]{:S(2)}) %all-to-all-start) | async-done | bytes 2097184 | tf_op jit(solution)/shard_map/all_to_all | solution.py:23
  78.6 1.3 copy-done.2
  79.9 2.1 %pad_maximum_fusion = bf16[52,128,256]{2,1,0:T(8,128)(2,1)S(1)} fusion(bf16[8,128,256]{2,1,0:T(8,128)(2,1)} %copy-done.3, bf16[32,128,256]{2,1,0:T(8,128)(2,1)} %copy-done.2, bf16[12,128,256]{2,1,0:T(8,128)(2,1)} %bitcast.58), kind=kLoop, calls=%fused_computation.6 | loop fusion | flops 3407872 | bytes 6815744 | tf_op jit(solution)/shard_map/concatenate | solution.py:25
  82.0 8.2 %gather_fusion.2 = bf16[192,128,256]{2,1,0:T(8,128)(2,1)} fusion(bf16[52,128,256]{2,1,0:T(8,128)(2,1)S(1)} %pad_maximum_fusion, s32[1024]{0:T(1024)S(1)} %pad_clamp_fusion), kind=kCustom, calls=%fused_computation.2 | custom fusion | bytes 25166592 | tf_op jit(solution)/shard_map/gather | solution.py:27
  90.3 9.0 %fusion.11 = bf16[12,128,256]{2,1,0:T(8,128)(2,1)S(1)} fusion(f32[12,128,256]{2,1,0:T(8,128)} %bitcast.56, bf16[12,16,128,128]{3,2,1,0:T(8,128)(2,1)} %param.13, bf16[12,16,128,256]{3,2,1,0:T(8,128)(2,1)} %bitcast.55), kind=kOutput, calls=%fused_computation.14 | convolution fusion | flops 1611792384 | bytes 21233664 | tf_op jit(solution)/shard_map/tkij,tkjh->tih/dot_general | solution.py:28
  99.3 1.5 fusion.27
  100.8 14.5 %fusion.28 = f32[12,256,16,128]{1,2,0,3:T(8,128)} fusion(bf16[12,128,256,1]{2,1,0,3:T(8,128)(2,1)S(1)} %bitcast.60, bf16[12,16,128,128]{2,1,0,3:T(8,128)(2,1)} %copy.11), kind=kOutput, calls=%fused_computation.41 | convolution fusion | flops 1610612736 | bytes 32243712 | tf_op jit(solution)/shard_map/tkij,tih->tkjh/dot_general | solution.py:42
  115.3 17.0 %bitcast_convert_fusion = bf16[52,128,256]{2,0,1:T(8,128)(2,1)} fusion(f32[12,256,16,128]{1,2,0,3:T(8,128)} %fusion.28, s32[12,16]{1,0:T(8,128)S(1)} %copy-done.6), kind=kOutput, calls=%fused_computation.5 | convolution fusion | flops 3927582464 | bytes 28574464 | tf_op jit(solution)/shard_map/tks,tkjh->sjh/dot_general | solution.py:44
  132.3 1.4 slice.15
  133.7 0.9 copy.14
  134.6 6.3 %all-to-all-start.3 = ((bf16[8,128,256]{2,1,0:T(8,128)(2,1)}), bf16[8,128,256]{2,1,0:T(8,128)(2,1)S(1)}, u32[]{:S(2)}, u32[]{:S(2)}) async-start(bf16[8,128,256]{2,1,0:T(8,128)(2,1)} %copy.14), calls=%async_computation.3 | async-start | bytes 1048576 | tf_op jit(solution)/shard_map/all_to_all | solution.py:50
  140.9 2.9 %slice.14 = bf16[32,128,256]{2,0,1:T(8,128)(2,1)S(1)} slice(bf16[52,128,256]{2,0,1:T(8,128)(2,1)} %bitcast_convert_fusion), slice={[12:44], [0:128], [0:256]} | slice | bytes 4194304 | tf_op jit(solution)/shard_map/slice | solution.py:48
  143.8 2.5 %copy.12 = bf16[32,128,256]{2,1,0:T(8,128)(2,1)} copy(bf16[32,128,256]{2,0,1:T(8,128)(2,1)S(1)} %slice.14) | data formatting | bytes 4194304 | tf_op jit(solution)/shard_map/slice | solution.py:48
  146.3 4.0 %all-to-all-done.3 = bf16[8,128,256]{2,1,0:T(8,128)(2,1)S(1)} async-done(((bf16[8,128,256]{2,1,0:T(8,128)(2,1)}), bf16[8,128,256]{2,1,0:T(8,128)(2,1)S(1)}, u32[]{:S(2)}, u32[]{:S(2)}) %all-to-all-start.3) | async-done | bytes 524320 | tf_op jit(solution)/shard_map/all_to_all | solution.py:50
  150.3 5.6 %all-to-all-start.2 = ((bf16[32,128,256]{2,1,0:T(8,128)(2,1)}), bf16[32,128,256]{2,1,0:T(8,128)(2,1)S(1)}, u32[]{:S(2)}, u32[]{:S(2)}) async-start(bf16[32,128,256]{2,1,0:T(8,128)(2,1)} %copy.12), calls=%async_computation.2 | async-start | bytes 4194304 | tf_op jit(solution)/shard_map/all_to_all | solution.py:47
  155.9 0.7 fusion.25
  156.6 0.7 fusion.26
  157.3 1.9 fusion.12
  159.2 44.9 %all-to-all-done.2 = bf16[32,128,256]{2,1,0:T(8,128)(2,1)S(1)} async-done(((bf16[32,128,256]{2,1,0:T(8,128)(2,1)}), bf16[32,128,256]{2,1,0:T(8,128)(2,1)S(1)}, u32[]{:S(2)}, u32[]{:S(2)}) %all-to-all-start.2) | async-done | bytes 2097184 | tf_op jit(solution)/shard_map/all_to_all | solution.py:47
  204.2 3.0 %fusion.8 = f32[12,128,256]{2,0,1:T(8,128)S(1)} fusion(f32[12,128,256]{2,0,1:T(8,128)} %fusion.12, bf16[32,128,256]{2,1,0:T(8,128)(2,1)S(1)} %all-to-all-done.2, s32[32]{0:T(128)S(1)} %fusion.25), kind=kOutput, calls=%fused_computation.12 | convolution fusion | flops 25559424 | bytes 5243008 | tf_op jit(solution)/shard_map/gl,gjh->ljh/dot_general | solution.py:56
  207.1 2.1 copy.16
  (17 shorter events, 0.5 us)
Async XLA Ops:
  0.6 1.2 copy-start
  3.2 16.0 %all-to-all-start.1 = ((bf16[8,128,256]{2,1,0:T(8,128)(2,1)}), bf16[8,128,256]{2,1,0:T(8,128)(2,1)S(1)}, u32[]{:S(2)}, u32[]{:S(2)}) async-start(bf16[8,128,256]{2,1,0:T(8,128)(2,1)} %gather_fusion.1), calls=%async_computation.1 | async-start | bytes 1048576 | tf_op jit(solution)/shard_map/all_to_all | solution.py:24
  12.5 17.9 %copy-start.6 = (s32[12,16]{1,0:T(8,128)S(1)}, s32[12,16]{1,0:T(8,128)}, u32[]{:S(2)}) copy-start(s32[12,16]{1,0:T(8,128)} %param.12) | copy-start | bytes 2308
  19.1 0.8 copy-start.3
  19.9 58.6 %all-to-all-start = ((bf16[32,128,256]{2,1,0:T(8,128)(2,1)}), bf16[32,128,256]{2,1,0:T(8,128)(2,1)S(1)}, u32[]{:S(2)}, u32[]{:S(2)}) async-start(bf16[32,128,256]{2,1,0:T(8,128)(2,1)} %gather_fusion), calls=%async_computation | async-start | bytes 4194304 | tf_op jit(solution)/shard_map/all_to_all | solution.py:23
  32.8 9.2 %copy-start.4 = (bf16[1536,256]{1,0:T(8,128)(2,1)S(1)}, bf16[1536,256]{1,0:T(8,128)(2,1)}, u32[]{:S(2)}) copy-start(bf16[1536,256]{1,0:T(8,128)(2,1)} %param.9) | copy-start | bytes 2359300
  78.6 1.3 copy-start.2
  90.3 9.0 %copy-start.5 = (bf16[256,256]{1,0:T(8,128)(2,1)S(1)}, bf16[256,256]{1,0:T(8,128)(2,1)}, u32[]{:S(2)}) copy-start(bf16[256,256]{1,0:T(8,128)(2,1)} %param.11) | copy-start | bytes 393220
  134.6 15.7 %all-to-all-start.3 = ((bf16[8,128,256]{2,1,0:T(8,128)(2,1)}), bf16[8,128,256]{2,1,0:T(8,128)(2,1)S(1)}, u32[]{:S(2)}, u32[]{:S(2)}) async-start(bf16[8,128,256]{2,1,0:T(8,128)(2,1)} %copy.14), calls=%async_computation.3 | async-start | bytes 1048576 | tf_op jit(solution)/shard_map/all_to_all | solution.py:50
  150.3 53.9 %all-to-all-start.2 = ((bf16[32,128,256]{2,1,0:T(8,128)(2,1)}), bf16[32,128,256]{2,1,0:T(8,128)(2,1)S(1)}, u32[]{:S(2)}, u32[]{:S(2)}) async-start(bf16[32,128,256]{2,1,0:T(8,128)(2,1)} %copy.12), calls=%async_computation.2 | async-start | bytes 4194304 | tf_op jit(solution)/shard_map/all_to_all | solution.py:47
  204.2 5.0 %copy-start.1 = (bf16[1536,256]{1,0:T(8,128)(2,1)S(1)}, bf16[1536,256]{1,0:T(8,128)(2,1)}, u32[]{:S(2)}) copy-start(bf16[1536,256]{1,0:T(8,128)(2,1)} %param.10) | copy-start | bytes 2359300
where the time goes:
time: 211 us; the launch traced here: 209 us
  waiting for transfers between devices  90.9 us (43%)
  matrix products  46.9 us (22%)
  local copies, waits for them, and re-layouts  34.5 us (16%)
  starting transfers between devices  28.9 us (14%)
  other arithmetic  7.27 us (3%)
    all_to_all x1, waiting for transfers between devices, body(): lax.all_to_all(messages[tiles:tiles + group_count], 'grp', split_axis=0,...  44.9 us
    all_to_all x1, waiting for transfers between devices, body(): lax.all_to_all(stale[serve_group], 'grp', split_axis=0, concat_axis=0, ti...  35.3 us
    dot_general x1, matrix products, body(): jnp.einsum('tks,tkjh->sjh', selector, each, precision=lax.Precision.HIGHEST)  17 us
    dot_general x1, matrix products, body(): jnp.einsum('tkij,tih->tkjh', block_values, outgoing, preferred_element_ty...  14.5 us
    unnamed x15, local copies, waits for them, and re-layouts  11.7 us
    all_to_all x1, starting transfers between devices, body(): lax.all_to_all(stale[serve_group], 'grp', split_axis=0, concat_axis=0, ti...  10.4 us
    dot_general x1, matrix products, body(): jnp.einsum('tkij,tkjh->tih', block_values, picked, preferred_element_type...  8.96 us
    gather x1, local copies, waits for them, and re-layouts, body(): picked = sources[column_ids]  8.23 us
  transfers between devices with their start and end apart: 4, of which 4 were waited for; matrix products, arithmetic and copies ran while one was open for 12% of the time, Pallas kernels for 0%

commit v1 on v0

v1 whole, which is shorter than its diff:
```python
import jax
import jax.numpy as jnp
from jax import lax
from jax.experimental import pallas as pl
from jax.experimental.pallas import tpu as pltpu
from jax.sharding import PartitionSpec as P

MESH = pl.DeviceIdType.MESH
teleport = 0.1
mapping_share = 0.5

TILES, ENTRIES, EDGE, HIDDEN = 12, 16, 128, 256
N_Z, N_Y, N_X, N_CORE = 8, 4, 4, 2
N_GRP, N_BLK = N_Z * N_Y, N_X * N_CORE
N_FAR = N_GRP + N_BLK
CHUNK = 4
OWN_CHUNKS, LOOP_CHUNKS, GROUP_CHUNKS = TILES // CHUNK, N_BLK // CHUNK, N_GRP // CHUNK
ROWS = TILES * EDGE
NONE = TILES * ENTRIES


def far_first(k, n):
    return lax.rem(n // 2 + (1 - 2 * lax.rem(k, 2)) * lax.div(k + 1, 2) + n, n)


def kernel(
    feat_h, init_h, hist_h, w_ref, ids_ref, val_h, gt_ref, lt_ref,
    refreshed_h, inbox_h,
    hist_v, feat_v, init_v, own_v, val_v, chain_v, turned_v, adj_v, send_v, pull_v, push_v,
    gath_v, out_v, left_v, box_v, last_v, prev_v, last_s, prev_s,
    in_sem, tab_sem, send_sem, recv_sem, send2_sem, recv2_sem, res_sem,
):
    f32, bf16 = jnp.float32, jnp.bfloat16
    g, b = lax.axis_index("grp"), lax.axis_index("blk")
    z, y = lax.div(g, N_Y), lax.rem(g, N_Y)
    x, core = lax.div(b, N_CORE), lax.rem(b, N_CORE)

    def group_at(i, sign):
        dz, dy = far_first(lax.div(i, N_Y), N_Z), far_first(lax.rem(i, N_Y), N_Y)
        return lax.rem(z + sign * dz + N_Z, N_Z) * N_Y + lax.rem(y + sign * dy + N_Y, N_Y)

    def loop_at(i, sign):
        dx, dc = far_first(lax.div(i, N_CORE), N_X), 1 - lax.rem(i, N_CORE)
        return lax.rem(x + sign * dx + N_X, N_X) * N_CORE + lax.rem(core + dc, N_CORE)

    def loop(lo, hi, body):
        def step(i, carry):
            body(i)
            return carry

        lax.fori_loop(lo, hi, step, 0)

    def group_copy(i, landing, ss, rs):
        return pltpu.make_async_remote_copy(
            src_ref=send_v.at[i], dst_ref=landing.at[i], send_sem=ss.at[i], recv_sem=rs.at[i],
            device_id={"grp": group_at(i, 1)}, device_id_type=MESH,
        )

    def loop_copy(i, landing, ss, rs):
        return pltpu.make_async_remote_copy(
            src_ref=send_v.at[N_GRP + i], dst_ref=landing.at[N_GRP + i],
            send_sem=ss.at[N_GRP + i], recv_sem=rs.at[N_GRP + i],
            device_id={"blk": loop_at(i, 1)}, device_id_type=MESH,
        )

    fetch_hist = pltpu.make_async_copy(hist_h, hist_v, in_sem.at[0])
    fetch_val = pltpu.make_async_copy(val_h, val_v.at[pl.ds(0, NONE)], in_sem.at[1])
    fetch_feat = pltpu.make_async_copy(feat_h, feat_v, in_sem.at[2])
    fetch_init = pltpu.make_async_copy(init_h, init_v, in_sem.at[3])
    fetch_hist.start()
    barrier = pltpu.get_barrier_semaphore()

    def greet_group(i):
        pl.semaphore_signal(barrier, inc=1, device_id={"grp": group_at(i, 1)}, device_id_type=MESH)

    def greet_loop(i):
        pl.semaphore_signal(barrier, inc=1, device_id={"blk": loop_at(i, 1)}, device_id_type=MESH)

    loop(0, N_GRP - 1, greet_group)
    loop(0, N_BLK - 1, greet_loop)
    fetch_val.start()
    fetch_feat.start()
    fetch_init.start()

    ids = ids_ref[...]
    wide = (TILES, 128)
    tile = lax.broadcasted_iota(jnp.int32, wide, 0)
    slot = lax.broadcasted_iota(jnp.int32, wide, 1)
    entry = lax.broadcasted_iota(jnp.int32, ids.shape, 1)
    last = jnp.full(wide, NONE, jnp.int32)
    prev = jnp.full(ids.shape, ENTRIES, jnp.int32)
    for k in range(ENTRIES):
        column = ids[:, k : k + 1]
        last = jnp.where(column == slot, tile * ENTRIES + k, last)
        prev = jnp.where(jnp.logical_and(column == ids, entry > k), k, prev)
    last_v[...] = jnp.zeros_like(last_v)
    prev_v[...] = jnp.zeros_like(prev_v)
    last_v[pl.ds(0, TILES), :] = last
    prev_v[pl.ds(0, TILES), pl.ds(0, ENTRIES)] = prev
    put_last = pltpu.make_async_copy(last_v, last_s, tab_sem.at[0])
    put_prev = pltpu.make_async_copy(prev_v, prev_s, tab_sem.at[1])
    put_last.start()
    put_prev.start()

    fetch_hist.wait()

    def stage_group(i):
        send_v[i] = hist_v[gt_ref[g, group_at(i, 1)]]

    def stage_loop(i):
        send_v[N_GRP + i] = hist_v[lt_ref[b, loop_at(i, 1)]]

    loop(0, N_GRP - 1, stage_group)
    loop(0, N_BLK - 1, stage_loop)
    pull_v[N_GRP - 1] = hist_v[gt_ref[g, g]]
    pull_v[N_FAR - 1] = hist_v[lt_ref[b, b]]
    put_last.wait()
    put_prev.wait()

    pl.semaphore_wait(barrier, N_GRP + N_BLK - 2)
    loop(0, N_GRP - 1, lambda i: group_copy(i, pull_v, send_sem, recv_sem).start())
    loop(0, N_BLK - 1, lambda i: loop_copy(i, pull_v, send_sem, recv_sem).start())

    fetch_val.wait()
    val_v[NONE] = jnp.zeros((EDGE, EDGE), bf16)
    turned_v[NONE] = jnp.zeros((EDGE, EDGE), bf16)
    chain_v[ENTRIES] = jnp.zeros((EDGE, EDGE), f32)

    def chain_tile(t):
        def chain_entry(k):
            e = t * ENTRIES + k
            total = val_v[e].astype(f32) + chain_v[prev_s[t, k]]
            chain_v[k] = total
            val_v[e] = total.astype(bf16)
            turned_v[e] = jnp.transpose(total).astype(bf16)

        loop(0, ENTRIES, chain_entry)

    loop(0, TILES, chain_tile)

    def lay_out(chunk, slot_of):
        def lay_tile(t):
            rows = pl.ds(pl.multiple_of(t * EDGE, EDGE), EDGE)
            for q in range(CHUNK):
                adj_v[chunk, rows, pl.ds(q * EDGE, EDGE)] = val_v[last_s[t, slot_of(q)]]

        loop(0, TILES, lay_tile)

    def group_slot(i, sign):
        return TILES + group_at(i, sign)

    def loop_slot(i, sign):
        return TILES + N_GRP + loop_at(i, sign)

    loop(0, OWN_CHUNKS, lambda m: lay_out(m, lambda q: m * CHUNK + q))
    loop(0, LOOP_CHUNKS, lambda m: lay_out(OWN_CHUNKS + m, lambda q: loop_slot(m * CHUNK + q, -1)))
    loop(0, GROUP_CHUNKS, lambda m: lay_out(OWN_CHUNKS + LOOP_CHUNKS + m, lambda q: group_slot(m * CHUNK + q, -1)))

    fetch_feat.wait()
    fetch_init.wait()

    def own_block(t):
        own_v[t] = feat_v[t].astype(bf16)
        gath_v[t] = jnp.zeros((EDGE, HIDDEN), f32)

    loop(0, TILES, own_block)

    def gather(chunk, blocks_ref, first):
        right = blocks_ref[pl.ds(first, CHUNK)].reshape(CHUNK * EDGE, HIDDEN)

        def gather_rows(m):
            rows = pl.ds(pl.multiple_of(m * CHUNK * EDGE, CHUNK * EDGE), CHUNK * EDGE)
            part = jnp.dot(adj_v[chunk, rows, :], right, preferred_element_type=f32)
            gath_v[pl.ds(m * CHUNK, CHUNK)] += part.reshape(CHUNK, EDGE, HIDDEN)

        loop(0, TILES // CHUNK, gather_rows)

    loop(0, OWN_CHUNKS, lambda m: gather(m, own_v, m * CHUNK))
    loop(0, N_BLK - 1, lambda i: loop_copy(i, pull_v, send_sem, recv_sem).wait_recv())
    loop(0, LOOP_CHUNKS, lambda m: gather(OWN_CHUNKS + m, pull_v, N_GRP + m * CHUNK))

    def gather_group(m):
        loop(m * CHUNK, m * CHUNK + CHUNK, lambda i: group_copy(i, pull_v, send_sem, recv_sem).wait_recv())
        gather(OWN_CHUNKS + LOOP_CHUNKS + m, pull_v, m * CHUNK)

    loop(0, GROUP_CHUNKS - 1, gather_group)
    final = (GROUP_CHUNKS - 1) * CHUNK
    loop(final, N_GRP - 1, lambda i: group_copy(i, pull_v, send_sem, recv_sem).wait_recv())
    gather(OWN_CHUNKS + LOOP_CHUNKS + GROUP_CHUNKS - 1, pull_v, final)

    def layer(m):
        start = init_v[pl.ds(m * CHUNK, CHUNK)].astype(f32)
        mixed = ((1.0 - teleport) * gath_v[pl.ds(m * CHUNK, CHUNK)] + teleport * start).astype(bf16)
        mixed = mixed.reshape(CHUNK * EDGE, HIDDEN)
        product = jnp.dot(mixed, w_ref[...], preferred_element_type=f32)
        fresh = jnp.maximum((1.0 - mapping_share) * mixed.astype(f32) + mapping_share * product, 0.0)
        out_v[pl.ds(m * CHUNK, CHUNK)] = fresh.reshape(CHUNK, EDGE, HIDDEN)
        left_v[pl.ds(pl.multiple_of(m * CHUNK * EDGE, CHUNK * EDGE), CHUNK * EDGE), :] = fresh.astype(bf16)

    loop(0, TILES // CHUNK, layer)
    loop(0, N_GRP - 1, lambda i: group_copy(i, pull_v, send_sem, recv_sem).wait_send())
    loop(0, N_BLK - 1, lambda i: loop_copy(i, pull_v, send_sem, recv_sem).wait_send())

    def message(c):
        left = jnp.concatenate([turned_v[last_s[t, c]] for t in range(TILES)], axis=1)
        return jnp.dot(left, left_v[...], preferred_element_type=f32).astype(bf16)

    def send_group(i):
        send_v[i] = message(group_slot(i, 1))
        group_copy(i, push_v, send2_sem, recv2_sem).start()

    def send_loop(i):
        send_v[N_GRP + i] = message(loop_slot(i, 1))
        loop_copy(i, push_v, send2_sem, recv2_sem).start()

    loop(0, N_GRP - 1, send_group)
    loop(0, N_BLK - 1, send_loop)
    push_v[N_GRP - 1] = message(TILES + g)
    push_v[N_FAR - 1] = message(TILES + N_GRP + b)
    store_out = pltpu.make_async_copy(out_v, refreshed_h, res_sem.at[0])
    store_out.start()

    def clear(t):
        box_v[t] = jnp.zeros((EDGE, HIDDEN), f32)

    loop(0, TILES, clear)

    def deliver(first, owner_block):
        def deliver_block(t):
            total = box_v[t]
            for q in range(CHUNK):
                total = total + jnp.where(owner_block(q) == t, push_v[first + q].astype(f32), 0.0)
            box_v[t] = total

        loop(0, TILES, deliver_block)

    loop(0, N_BLK - 1, lambda i: loop_copy(i, push_v, send2_sem, recv2_sem).wait_recv())
    loop(0, LOOP_CHUNKS, lambda m: deliver(N_GRP + m * CHUNK, lambda q: lt_ref[b, loop_at(m * CHUNK + q, -1)]))

    def deliver_group(m):
        loop(m * CHUNK, m * CHUNK + CHUNK, lambda i: group_copy(i, push_v, send2_sem, recv2_sem).wait_recv())
        deliver(m * CHUNK, lambda q: gt_ref[g, group_at(m * CHUNK + q, -1)])

    loop(0, GROUP_CHUNKS - 1, deliver_group)
    loop(final, N_GRP - 1, lambda i: group_copy(i, push_v, send2_sem, recv2_sem).wait_recv())
    deliver(final, lambda q: gt_ref[g, group_at(final + q, -1)])
    store_box = pltpu.make_async_copy(box_v, inbox_h, res_sem.at[1])
    store_box.start()
    loop(0, N_GRP - 1, lambda i: group_copy(i, push_v, send2_sem, recv2_sem).wait_send())
    loop(0, N_BLK - 1, lambda i: loop_copy(i, push_v, send2_sem, recv2_sem).wait_send())
    store_out.wait()
    store_box.wait()


def body(features, initial, history, weight, column_ids, block_values, group_table, loop_table):
    f32, bf16, i32 = jnp.float32, jnp.bfloat16, jnp.int32
    blocks = (TILES, EDGE, HIDDEN)
    any_space = pl.BlockSpec(memory_space=pl.ANY)
    vmem, smem = pl.BlockSpec(memory_space=pltpu.VMEM), pl.BlockSpec(memory_space=pltpu.SMEM)
    dma = pltpu.SemaphoreType.DMA
    refreshed, inbox = pl.pallas_call(
        kernel,
        out_shape=[jax.ShapeDtypeStruct(blocks, f32)] * 2,
        in_specs=[any_space, any_space, any_space, vmem, vmem, any_space, smem, smem],
        out_specs=[any_space, any_space],
        scratch_shapes=[
            pltpu.VMEM(blocks, bf16),
            pltpu.VMEM(blocks, f32),
            pltpu.VMEM(blocks, bf16),
            pltpu.VMEM(blocks, bf16),
            pltpu.VMEM((NONE + 1, EDGE, EDGE), bf16),
            pltpu.VMEM((ENTRIES + 1, EDGE, EDGE), f32),
            pltpu.VMEM((NONE + 1, EDGE, EDGE), bf16),
            pltpu.VMEM((OWN_CHUNKS + LOOP_CHUNKS + GROUP_CHUNKS, ROWS, CHUNK * EDGE), bf16),
            pltpu.VMEM((N_FAR, EDGE, HIDDEN), bf16),
            pltpu.VMEM((N_FAR, EDGE, HIDDEN), bf16),
            pltpu.VMEM((N_FAR, EDGE, HIDDEN), bf16),
            pltpu.VMEM(blocks, f32),
            pltpu.VMEM(blocks, f32),
            pltpu.VMEM((ROWS, HIDDEN), bf16),
            pltpu.VMEM(blocks, f32),
            pltpu.VMEM((16, 128), i32),
            pltpu.VMEM((16, 128), i32),
            pltpu.SMEM((16, 128), i32),
            pltpu.SMEM((16, 128), i32),
            dma((4,)),
            dma((2,)),
            dma((N_FAR,)),
            dma((N_FAR,)),
            dma((N_FAR,)),
            dma((N_FAR,)),
            dma((2,)),
        ],
        compiler_params=pltpu.CompilerParams(
            collective_id=0, has_side_effects=True, vmem_limit_bytes=64 * 2**20 - 2**16
        ),
    )(
        features.reshape(blocks),
        initial.reshape(blocks),
        history.reshape(blocks),
        weight,
        column_ids,
        block_values.reshape(NONE, EDGE, EDGE),
        group_table[0],
        loop_table[0],
    )
    return refreshed.reshape(ROWS, HIDDEN), inbox.reshape(ROWS, HIDDEN)


def solution(mesh):
    in_specs = (
        P(("blk", "grp"), None),
        P(("blk", "grp"), None),
        P(("blk", "grp"), None),
        P(),
        P(("blk", "grp"), None),
        P(("blk", "grp"), None, None, None),
        P("blk", None, None),
        P("grp", None, None),
    )
    out_specs = (P(("blk", "grp"), None), P(("blk", "grp"), None))
    return jax.shard_map(body, mesh=mesh, in_specs=in_specs, out_specs=out_specs, check_vma=False)
```

time: 211 us -> 122 us (0.58)
  Pallas kernels: 0 us -> 117 us
  waiting for transfers between devices: 90.9 us -> 0 us
  matrix products: 46.9 us -> 0 us
  local copies, waits for them, and re-layouts: 34.5 us -> 3.92 us
  starting transfers between devices: 28.9 us -> 0 us
  other arithmetic: 7.27 us -> 0 us
    pallas_call x0 -> x1, Pallas kernels: none -> 117 us  [body(): pl.pallas_call(kernel, out_shape=[jax.ShapeDtypeStruct(blocks, f32)] * 2,...]
    all_to_all x4 -> x0, waiting for transfers between devices: 90.9 us -> none  [the longest x1 44.9 us: body(): lax.all_to_all(messages[tiles:tiles + group_count], 'grp', split_axis=0,...]
    dot_general x6 -> x0, matrix products: 46.9 us -> none  [the longest x1 17 us: body(): jnp.einsum('tks,tkjh->sjh', selector, each, precision=lax.Precision.HIGHEST)]
    all_to_all x4 -> x0, starting transfers between devices: 28.9 us -> none  [the longest x1 10.4 us: body(): lax.all_to_all(stale[serve_group], 'grp', split_axis=0, concat_axis=0, ti...]
    gather x3 -> x0, local copies, waits for them, and re-layouts: 11.6 us -> none  [the longest x1 8.23 us: body(): picked = sources[column_ids]]
    unnamed x15 -> x4, local copies, waits for them, and re-layouts: 11.7 us -> 3.92 us
    slice x4 -> x0, local copies, waits for them, and re-layouts: 7.69 us -> none  [the longest x2 5.4 us: body(): messages[tiles:tiles + group_count]]
    convert_element_type x1 -> x0, other arithmetic: 2.37 us -> none  [body(): own_blocks = features.astype(jnp.bfloat16).reshape(tiles, edge, hidden)]
  transfers between devices with their start and end apart: 4 -> 0, of which waited for: 4 -> 0; matrix products, arithmetic and copies ran while one was open for 12% -> 0% of each run, Pallas kernels for 0% -> 0%
where the time goes in v1:
time: 122 us
  Pallas kernels  117 us (96%)
  local copies, waits for them, and re-layouts  3.92 us (3%)
    pallas_call x1, Pallas kernels, body(): pl.pallas_call(kernel, out_shape=[jax.ShapeDtypeStruct(blocks, f32)] * 2,...  117 us
    unnamed x4, local copies, waits for them, and re-layouts  3.92 us

profile of v1, /device:TPU:1, one launch (start us, length us, event | category | flops | bytes accessed | tf_op | source)
XLA Modules:
  0.0 121.6 jit_solution(5664175611624760410)
XLA Ops:
  0.6 117.1 %shard_map.95 = (f32[12,128,256]{2,1,0:T(8,128)}, f32[12,128,256]{2,1,0:T(8,128)}) custom-call(f32[12,128,256]{2,1,0:T(8,128)} %bitcast.9, bf16[12,128,256]{2,1,0:T(8,128)(2,1)} %bitcast.12, bf16[12,128,256]{2,1,0:T(8,128)(2,1)} %bitcast.13, bf16[256,256]{1,0:T(8,128)(2,1)} %w_ref.1, s32[12,16]{1,0:T(8,128)} %ids_ref.1, bf16[192,128,128]{2,1,0:T(8,128)(2,1)} %bitcast.8, ...), custom_call_target="tpu_custom_call" | custom-call | tf_op jit(solution)/shard_map/pallas_call | solution.py:261
  117.7 0.0 copy-start
  117.7 2.8 %copy.12 = f32[1536,256]{1,0:T(8,128)} copy(f32[1536,256]{1,0:T(8,128)} %bitcast.11) | data formatting | bytes 3145728
  120.5 0.0 copy-done
  120.5 1.1 copy.13
Async XLA Ops:
  117.7 2.8 %copy-start = (f32[12,128,256]{2,1,0:T(8,128)S(1)}, f32[12,128,256]{2,1,0:T(8,128)}, u32[]{:S(2)}) copy-start(f32[12,128,256]{2,1,0:T(8,128)} %get-tuple-element.5) | copy-start | bytes 4718596

commit v2 on v1

v2 whole, which is shorter than its diff:
```python
import jax
import jax.numpy as jnp
from jax import lax
from jax.experimental import pallas as pl
from jax.experimental.pallas import tpu as pltpu
from jax.sharding import PartitionSpec as P

MESH = pl.DeviceIdType.MESH
teleport = 0.1
mapping_share = 0.5

TILES, ENTRIES, EDGE, HIDDEN = 12, 16, 128, 256
N_Z, N_Y, N_X, N_CORE = 8, 4, 4, 2
N_GRP, N_BLK = N_Z * N_Y, N_X * N_CORE
N_FAR = N_GRP + N_BLK
SELF = N_Z - 1
Y_LINE = N_GRP - (N_Y - 1)
PAIR = 2
OWN_PAIRS, LOOP_PAIRS, GROUP_PAIRS = TILES // PAIR, N_BLK // PAIR, N_GRP // PAIR
BAND = 6
ROWS = TILES * EDGE
NONE = TILES * ENTRIES


def far_first(k, n):
    return lax.rem(n // 2 + (1 - 2 * lax.rem(k, 2)) * lax.div(k + 1, 2) + n, n)


def kernel(
    feat_h, init_h, hist_h, w_h, ids_h, val_h, gt_h, lt_h,
    out_v, box_v,
    hist_v, init_v, w_v, ids_v, own_v, val_v, low_v, chain_v, adj_v, send_v, pull_v, push_v,
    left_v, last_v, prev_v, last_s, prev_s, gt_s, lt_s,
    in_sem, tab_sem, line_sem, send_sem, recv_sem, send2_sem, recv2_sem,
):
    f32, bf16 = jnp.float32, jnp.bfloat16
    g, b = lax.axis_index("grp"), lax.axis_index("blk")
    z, y = lax.div(g, N_Y), lax.rem(g, N_Y)
    x, core = lax.div(b, N_CORE), lax.rem(b, N_CORE)
    gath_v = box_v

    def group_of(dz, dy, sign):
        return lax.rem(z + sign * dz + N_Z, N_Z) * N_Y + lax.rem(y + sign * dy + N_Y, N_Y)

    def group_at(i, sign):
        r = jnp.maximum(i - N_Z, 0)
        on_z, on_y = i < N_Z, i >= Y_LINE
        dz = jnp.where(on_z, far_first(i, N_Z), jnp.where(on_y, 0, far_first(lax.div(r, N_Y - 1), N_Z)))
        dy = jnp.where(on_z, 0, far_first(lax.rem(r, N_Y - 1), N_Y))
        return group_of(dz, dy, sign)

    def loop_at(i, sign):
        dx, dc = far_first(lax.div(i, N_CORE), N_X), 1 - lax.rem(i, N_CORE)
        return lax.rem(x + sign * dx + N_X, N_X) * N_CORE + lax.rem(core + dc, N_CORE)

    def loop(lo, hi, body, unroll=1):
        def step(i, carry):
            for u in range(unroll):
                body(lo + i * unroll + u)
            return carry

        lax.fori_loop(0, (hi - lo) // unroll, step, 0)

    def group_copy(i, landing, ss, rs):
        return pltpu.make_async_remote_copy(
            src_ref=send_v.at[i], dst_ref=landing.at[i], send_sem=ss.at[i], recv_sem=rs.at[i],
            device_id={"grp": group_at(i, 1)}, device_id_type=MESH,
        )

    def loop_copy(i, landing, ss, rs):
        return pltpu.make_async_remote_copy(
            src_ref=send_v.at[N_GRP + i], dst_ref=landing.at[N_GRP + i],
            send_sem=ss.at[N_GRP + i], recv_sem=rs.at[N_GRP + i],
            device_id={"blk": loop_at(i, 1)}, device_id_type=MESH,
        )

    fetch_hist = pltpu.make_async_copy(hist_h, hist_v, in_sem.at[0])
    fetch_gt = pltpu.make_async_copy(gt_h, gt_s, in_sem.at[1])
    fetch_lt = pltpu.make_async_copy(lt_h, lt_s, in_sem.at[2])
    fetch_ids = pltpu.make_async_copy(ids_h, ids_v, in_sem.at[3])
    fetch_val = pltpu.make_async_copy(val_h, val_v.at[pl.ds(0, NONE)], in_sem.at[4])
    fetch_feat = pltpu.make_async_copy(feat_h, out_v, in_sem.at[5])
    fetch_init = pltpu.make_async_copy(init_h, init_v, in_sem.at[6])
    fetch_w = pltpu.make_async_copy(w_h, w_v, in_sem.at[7])
    for fetch in (fetch_gt, fetch_lt, fetch_hist, fetch_ids):
        fetch.start()
    barrier = pltpu.get_barrier_semaphore()

    def greet_group(i):
        pl.semaphore_signal(barrier, inc=1, device_id={"grp": group_at(i, 1)}, device_id_type=MESH)

    def greet_loop(i):
        pl.semaphore_signal(barrier, inc=1, device_id={"blk": loop_at(i, 1)}, device_id_type=MESH)

    loop(0, SELF, greet_group)
    loop(Y_LINE, N_GRP, greet_group)
    loop(0, N_BLK - 1, greet_loop)
    for fetch in (fetch_val, fetch_feat, fetch_init, fetch_w):
        fetch.start()

    fetch_gt.wait()
    fetch_lt.wait()
    fetch_hist.wait()

    def stage_group(i):
        send_v[i] = hist_v[gt_s[g, group_at(i, 1)]]

    def stage_loop(i):
        send_v[N_GRP + i] = hist_v[lt_s[b, loop_at(i, 1)]]

    loop(0, SELF, stage_group)
    loop(SELF + 1, N_GRP, stage_group)
    loop(0, N_BLK - 1, stage_loop)
    pull_v[SELF] = hist_v[gt_s[g, g]]
    pull_v[N_FAR - 1] = hist_v[lt_s[b, b]]

    def pull_group(i):
        group_copy(i, pull_v, send_sem, recv_sem).start()

    pl.semaphore_wait(barrier, (N_Z - 1) + (N_Y - 1) + (N_BLK - 1))

    def greet_line(i):
        pl.semaphore_signal(line_sem, inc=1, device_id={"grp": group_at(i, 1)}, device_id_type=MESH)

    loop(Y_LINE, N_GRP, greet_line)
    loop(0, SELF, pull_group)
    loop(Y_LINE, N_GRP, pull_group)
    loop(0, N_BLK - 1, lambda i: loop_copy(i, pull_v, send_sem, recv_sem).start())
    pl.semaphore_wait(line_sem, N_Y - 1)
    loop(N_Z, Y_LINE, pull_group)

    fetch_ids.wait()
    ids = ids_v[...]
    wide = (TILES, 128)
    tile = lax.broadcasted_iota(jnp.int32, wide, 0)
    slot = lax.broadcasted_iota(jnp.int32, wide, 1)
    entry = lax.broadcasted_iota(jnp.int32, ids.shape, 1)
    last = jnp.full(wide, NONE, jnp.int32)
    prev = jnp.full(ids.shape, ENTRIES, jnp.int32)
    for k in range(ENTRIES):
        column = ids[:, k : k + 1]
        last = jnp.where(column == slot, tile * ENTRIES + k, last)
        prev = jnp.where(jnp.logical_and(column == ids, entry > k), k, prev)
    last_v[...] = jnp.zeros_like(last_v)
    prev_v[...] = jnp.zeros_like(prev_v)
    last_v[pl.ds(0, TILES), :] = last
    prev_v[pl.ds(0, TILES), pl.ds(0, ENTRIES)] = prev
    put_last = pltpu.make_async_copy(last_v, last_s, tab_sem.at[0])
    put_prev = pltpu.make_async_copy(prev_v, prev_s, tab_sem.at[1])
    put_last.start()
    put_prev.start()
    put_last.wait()
    put_prev.wait()

    fetch_val.wait()
    for none in (val_v, low_v):
        none[NONE] = jnp.zeros((EDGE, EDGE), bf16)
    chain_v[ENTRIES] = jnp.zeros((EDGE, EDGE), f32)

    def chain_tile(t):
        def chain_entry(k):
            e = t * ENTRIES + k
            total = val_v[e].astype(f32) + chain_v[prev_s[t, k]]
            high = total.astype(bf16)
            chain_v[k] = total
            val_v[e] = high
            low_v[e] = (total - high.astype(f32)).astype(bf16)

        loop(0, ENTRIES, chain_entry, 4)

    loop(0, TILES, chain_tile)

    def group_slot(i, sign):
        return TILES + group_at(i, sign)

    def loop_slot(i, sign):
        return TILES + N_GRP + loop_at(i, sign)

    def lay_out(pair, first, second):
        def lay_tile(t):
            rows = pl.ds(pl.multiple_of(t * EDGE, EDGE), EDGE)
            for q, c in enumerate((first, second)):
                e = last_s[t, c]
                adj_v[pair, rows, pl.ds(q * EDGE, EDGE)] = val_v[e]
                adj_v[pair, rows, pl.ds((PAIR + q) * EDGE, EDGE)] = low_v[e]

        loop(0, TILES, lay_tile, 4)

    fetch_feat.wait()

    def own_block(t):
        own_v[t] = out_v[t].astype(bf16)
        gath_v[t] = jnp.zeros((EDGE, HIDDEN), f32)

    loop(0, TILES, own_block)

    def product_of(pair, blocks_ref, first, m):
        right = blocks_ref[pl.ds(first, PAIR)].reshape(PAIR * EDGE, HIDDEN)
        right = jnp.concatenate([right, right], axis=0)
        rows = pl.ds(pl.multiple_of(m * BAND * EDGE, BAND * EDGE), BAND * EDGE)
        part = jnp.dot(adj_v[pair, rows, :], right, preferred_element_type=f32)
        return part.reshape(BAND, EDGE, HIDDEN)

    def gather(pair, blocks_ref, first, pairs=1):
        def gather_rows(m):
            part = product_of(pair, blocks_ref, first, m)
            for extra in range(1, pairs):
                part = part + product_of(pair + extra, blocks_ref, first + extra * PAIR, m)
            gath_v[pl.ds(m * BAND, BAND)] += part

        loop(0, TILES // BAND, gather_rows)

    loop(0, OWN_PAIRS, lambda p: lay_out(p, p * PAIR, p * PAIR + 1))
    loop(0, OWN_PAIRS // 2, lambda p: gather(2 * p, own_v, 2 * p * PAIR, 2))
    loop(0, N_BLK - 1, lambda i: loop_copy(i, pull_v, send_sem, recv_sem).wait_recv())

    loop(0, LOOP_PAIRS, lambda p: lay_out(p, loop_slot(p * PAIR, -1), loop_slot(p * PAIR + 1, -1)))
    loop(0, LOOP_PAIRS // 2, lambda p: gather(2 * p, pull_v, N_GRP + 2 * p * PAIR, 2))
    loop(0, GROUP_PAIRS, lambda p: lay_out(p, group_slot(p * PAIR, -1), group_slot(p * PAIR + 1, -1)))
    fetch_init.wait()
    fetch_w.wait()

    def pulled_group(i):
        group_copy(i, pull_v, send_sem, recv_sem).wait_recv()

    def gather_group(p):
        loop(2 * p * PAIR, 2 * p * PAIR + 2 * PAIR, pulled_group)
        gather(2 * p, pull_v, 2 * p * PAIR, 2)

    loop(Y_LINE, N_GRP, pulled_group)
    gather(GROUP_PAIRS - 1, pull_v, N_GRP - PAIR)
    gather_group(0)
    loop(SELF - 3, SELF, pulled_group)
    gather(SELF // PAIR - 1, pull_v, SELF - 3, 2)
    loop(2, GROUP_PAIRS // 2 - 1, gather_group)
    pulled_group(Y_LINE - 1)

    def layer(m):
        gathered = gath_v[pl.ds(m * BAND, BAND)] + product_of(GROUP_PAIRS - 2, pull_v, Y_LINE - 1, m)
        start = init_v[pl.ds(m * BAND, BAND)].astype(f32)
        mixed = ((1.0 - teleport) * gathered + teleport * start).astype(bf16)
        mixed = mixed.reshape(BAND * EDGE, HIDDEN)
        product = jnp.dot(mixed, w_v[...], preferred_element_type=f32)
        fresh = jnp.maximum((1.0 - mapping_share) * mixed.astype(f32) + mapping_share * product, 0.0)
        out_v[pl.ds(m * BAND, BAND)] = fresh.reshape(BAND, EDGE, HIDDEN)
        left_v[pl.ds(pl.multiple_of(m * BAND * EDGE, BAND * EDGE), BAND * EDGE), :] = fresh.astype(bf16)

    loop(0, TILES // BAND, layer)

    def message(c):
        left = jnp.concatenate([val_v[last_s[t, c]] for t in range(TILES)], axis=0)
        total = lax.dot_general(left, left_v[...], (((0,), (0,)), ((), ())), preferred_element_type=f32)
        return total.astype(bf16)

    def send_group(i):
        group_copy(i, pull_v, send_sem, recv_sem).wait_send()
        send_v[i] = message(group_slot(i, 1))
        group_copy(i, push_v, send2_sem, recv2_sem).start()

    def send_loop(i):
        loop_copy(i, pull_v, send_sem, recv_sem).wait_send()
        send_v[N_GRP + i] = message(loop_slot(i, 1))
        loop_copy(i, push_v, send2_sem, recv2_sem).start()

    loop(0, SELF, send_group)
    loop(N_Z, N_GRP, send_group)
    loop(0, N_BLK - 1, send_loop)
    push_v[SELF] = message(TILES + g)
    push_v[N_FAR - 1] = message(TILES + N_GRP + b)

    def clear(t):
        box_v[t] = jnp.zeros((EDGE, HIDDEN), f32)

    loop(0, TILES, clear)

    def deliver(first, owner_block):
        owners = [owner_block(q) for q in range(PAIR)]

        def deliver_rows(r):
            rows = pl.ds(pl.multiple_of(r * 16, 16), 16)
            parts = [push_v[first + q, rows, :].astype(f32) for q in range(PAIR)]
            for t in range(TILES):
                total = box_v[t, rows, :]
                for q in range(PAIR):
                    total = total + jnp.where(owners[q] == t, parts[q], 0.0)
                box_v[t, rows, :] = total

        loop(0, EDGE // 16, deliver_rows)

    def pushed_group(i):
        group_copy(i, push_v, send2_sem, recv2_sem).wait_recv()

    def deliver_pair(p):
        deliver(p * PAIR, lambda q: gt_s[g, group_at(p * PAIR + q, -1)])

    def deliver_group(p):
        loop(p * PAIR, p * PAIR + PAIR, pushed_group)
        deliver_pair(p)

    loop(0, N_BLK - 1, lambda i: loop_copy(i, push_v, send2_sem, recv2_sem).wait_recv())
    loop(0, LOOP_PAIRS, lambda p: deliver(N_GRP + p * PAIR, lambda q: lt_s[b, loop_at(p * PAIR + q, -1)]))
    loop(Y_LINE, N_GRP, pushed_group)
    deliver_pair(GROUP_PAIRS - 1)
    loop(0, SELF // PAIR, deliver_group)
    pushed_group(SELF - 1)
    deliver_pair(SELF // PAIR)
    loop(N_Z // PAIR, GROUP_PAIRS - 2, deliver_group)
    pushed_group(Y_LINE - 1)
    deliver_pair(GROUP_PAIRS - 2)

    def sent_group(i):
        group_copy(i, push_v, send2_sem, recv2_sem).wait_send()

    loop(0, SELF, sent_group)
    loop(N_Z, N_GRP, sent_group)
    loop(0, N_BLK - 1, lambda i: loop_copy(i, push_v, send2_sem, recv2_sem).wait_send())


def body(features, initial, history, weight, column_ids, block_values, group_table, loop_table):
    f32, bf16, i32 = jnp.float32, jnp.bfloat16, jnp.int32
    blocks = (TILES, EDGE, HIDDEN)
    any_space, vmem = pl.BlockSpec(memory_space=pl.ANY), pl.BlockSpec(memory_space=pltpu.VMEM)
    dma = pltpu.SemaphoreType.DMA
    far = (N_FAR, EDGE, HIDDEN)
    refreshed, inbox = pl.pallas_call(
        kernel,
        out_shape=[pltpu.VMEM(blocks, f32)] * 2,
        in_specs=[any_space] * 8,
        out_specs=[vmem, vmem],
        scratch_shapes=[
            pltpu.VMEM(blocks, bf16),
            pltpu.VMEM(blocks, bf16),
            pltpu.VMEM((HIDDEN, HIDDEN), bf16),
            pltpu.VMEM((TILES, ENTRIES), i32),
            pltpu.VMEM(blocks, bf16),
            pltpu.VMEM((NONE + 1, EDGE, EDGE), bf16),
            pltpu.VMEM((NONE + 1, EDGE, EDGE), bf16),
            pltpu.VMEM((ENTRIES + 1, EDGE, EDGE), f32),
            pltpu.VMEM((GROUP_PAIRS, ROWS, 2 * PAIR * EDGE), bf16),
            pltpu.VMEM(far, bf16),
            pltpu.VMEM(far, bf16),
            pltpu.VMEM(far, bf16),
            pltpu.VMEM((ROWS, HIDDEN), bf16),
            pltpu.VMEM((16, 128), i32),
            pltpu.VMEM((16, 128), i32),
            pltpu.SMEM((16, 128), i32),
            pltpu.SMEM((16, 128), i32),
            pltpu.SMEM((N_GRP, N_GRP), i32),
            pltpu.SMEM((N_BLK, N_BLK), i32),
            dma((8,)),
            dma((2,)),
            pltpu.SemaphoreType.REGULAR,
            dma((N_FAR,)),
            dma((N_FAR,)),
            dma((N_FAR,)),
            dma((N_FAR,)),
        ],
        compiler_params=pltpu.CompilerParams(
            collective_id=0, has_side_effects=True, vmem_limit_bytes=60 * 2**20
        ),
    )(
        features.reshape(blocks),
        initial.reshape(blocks),
        history.reshape(blocks),
        weight,
        column_ids,
        block_values.reshape(NONE, EDGE, EDGE),
        group_table[0],
        loop_table[0],
    )
    return refreshed.reshape(ROWS, HIDDEN), inbox.reshape(ROWS, HIDDEN)


def solution(mesh):
    in_specs = (
        P(("blk", "grp"), None),
        P(("blk", "grp"), None),
        P(("blk", "grp"), None),
        P(),
        P(("blk", "grp"), None),
        P(("blk", "grp"), None, None, None),
        P("blk", None, None),
        P("grp", None, None),
    )
    out_specs = (P(("blk", "grp"), None), P(("blk", "grp"), None))
    return jax.shard_map(body, mesh=mesh, in_specs=in_specs, out_specs=out_specs, check_vma=False)
```

time: 122 us -> 114 us (0.934)
  Pallas kernels: 117 us -> 111 us
  local copies, waits for them, and re-layouts: 3.92 us -> 2.29 us
    pallas_call x1, Pallas kernels: 117 us -> 111 us  [body(): pl.pallas_call(kernel, out_shape=[pltpu.VMEM(blocks, f32)] * 2, in_specs=...]
    unnamed x4 -> x2, local copies, waits for them, and re-layouts: 3.92 us -> 2.29 us
where the time goes in v2:
time: 114 us
  Pallas kernels  111 us (97%)
  local copies, waits for them, and re-layouts  2.29 us (2%)
    pallas_call x1, Pallas kernels, body(): pl.pallas_call(kernel, out_shape=[pltpu.VMEM(blocks, f32)] * 2, in_specs=...  111 us
    unnamed x2, local copies, waits for them, and re-layouts  2.29 us

profile of v2, /device:TPU:1, one launch (start us, length us, event | category | flops | bytes accessed | tf_op | source)
XLA Modules:
  0.0 114.3 jit_solution(16904415164571403533)
XLA Ops:
  0.6 111.3 %shard_map.95 = (f32[12,128,256]{2,1,0:T(8,128)S(1)}, f32[12,128,256]{2,1,0:T(8,128)S(1)}) custom-call(f32[12,128,256]{2,1,0:T(8,128)} %bitcast.11, bf16[12,128,256]{2,1,0:T(8,128)(2,1)} %bitcast.12, bf16[12,128,256]{2,1,0:T(8,128)(2,1)} %bitcast.13, bf16[256,256]{1,0:T(8,128)(2,1)} %w_h.1, s32[12,16]{1,0:T(8,128)} %ids_h.1, ...), custom_call_target="tpu_custom_call" | custom-call | tf_op jit(solution)/shard_map/pallas_call | solution.py:325
  112.0 1.1 %copy.12 = f32[1536,256]{1,0:T(8,128)} copy(f32[1536,256]{1,0:T(8,128)S(1)} %bitcast.9) | data formatting | bytes 3145728
  113.1 1.1 copy.13

commit v3 on v2

--- a/solution.py
+++ b/solution.py
@@ -245,7 +245,7 @@
         out_v[pl.ds(m * BAND, BAND)] = fresh.reshape(BAND, EDGE, HIDDEN)
         left_v[pl.ds(pl.multiple_of(m * BAND * EDGE, BAND * EDGE), BAND * EDGE), :] = fresh.astype(bf16)
 
-    loop(0, TILES // BAND, layer)
+    loop(0, TILES // BAND, layer, 2)
 
     def message(c):
         left = jnp.concatenate([val_v[last_s[t, c]] for t in range(TILES)], axis=0)
@@ -314,6 +314,14 @@
     loop(0, SELF, sent_group)
     loop(N_Z, N_GRP, sent_group)
     loop(0, N_BLK - 1, lambda i: loop_copy(i, push_v, send2_sem, recv2_sem).wait_send())
+
+
+def put_out(out_v, box_v, out_h, box_h, sem):
+    copies = [pltpu.make_async_copy(out_v, out_h, sem.at[0]), pltpu.make_async_copy(box_v, box_h, sem.at[1])]
+    for copy in copies:
+        copy.start()
+    for copy in copies:
+        copy.wait()
 
 
 def body(features, initial, history, weight, column_ids, block_values, group_table, loop_table):
@@ -368,6 +376,15 @@
         group_table[0],
         loop_table[0],
     )
+    held = [pltpu.with_memory_space_constraint(array, pltpu.VMEM) for array in (refreshed, inbox)]
+    refreshed, inbox = pl.pallas_call(
+        put_out,
+        out_shape=[jax.ShapeDtypeStruct(blocks, f32)] * 2,
+        in_specs=[vmem] * 2,
+        out_specs=[any_space] * 2,
+        scratch_shapes=[dma((2,))],
+        compiler_params=pltpu.CompilerParams(vmem_limit_bytes=4 * 2**20),
+    )(*held)
     return refreshed.reshape(ROWS, HIDDEN), inbox.reshape(ROWS, HIDDEN)
 
 

time: 114 us -> 114 us (level)
  local copies, waits for them, and re-layouts: 2.29 us -> 0 us
  Pallas kernels: 111 us -> 113 us
    unnamed x2 -> x0, local copies, waits for them, and re-layouts: 2.29 us -> none
    pallas_call x0 -> x1, Pallas kernels: none -> 1.68 us  [body(): pl.pallas_call(put_out, out_shape=[jax.ShapeDtypeStruct(blocks, f32)] * 2...]
where the time goes in v3:
time: 114 us
  Pallas kernels  113 us (99%)
    pallas_call x1, Pallas kernels, body(): pl.pallas_call(kernel, out_shape=[pltpu.VMEM(blocks, f32)] * 2, in_specs=...  111 us

profile of v3, /device:TPU:1, one launch (start us, length us, event | category | flops | bytes accessed | tf_op | source)
XLA Modules:
  0.0 113.7 jit_solution(16224162338494661280)
XLA Ops:
  0.6 111.4 %shard_map.95 = (f32[12,128,256]{2,1,0:T(8,128)S(1)}, f32[12,128,256]{2,1,0:T(8,128)S(1)}) custom-call(f32[12,128,256]{2,1,0:T(8,128)} %bitcast.9, bf16[12,128,256]{2,1,0:T(8,128)(2,1)} %bitcast.10, bf16[12,128,256]{2,1,0:T(8,128)(2,1)} %bitcast.11, bf16[256,256]{1,0:T(8,128)(2,1)} %w_h.1, s32[12,16]{1,0:T(8,128)} %ids_h.1, bf16[192,128,128]{2,1,0:T(8,128)(2,1)} %bitcast.8, ...), custom_call_target="tpu_custom_call" | custom-call | tf_op jit(solution)/shard_map/pallas_call | solution.py:333
  112.0 1.7 %shard_map.96 = (f32[12,128,256]{2,1,0:T(8,128)}, f32[12,128,256]{2,1,0:T(8,128)}) custom-call(f32[12,128,256]{2,1,0:T(8,128)S(1)} %get-tuple-element.6.out_v, f32[12,128,256]{2,1,0:T(8,128)S(1)} %get-tuple-element.7.box_v), custom_call_target="tpu_custom_call" | custom-call | tf_op jit(solution)/shard_map/pallas_call | solution.py:380

commit v4 on v3

--- a/solution.py
+++ b/solution.py
@@ -262,8 +262,9 @@
         send_v[N_GRP + i] = message(loop_slot(i, 1))
         loop_copy(i, push_v, send2_sem, recv2_sem).start()
 
+    loop(N_Z, Y_LINE, send_group)
     loop(0, SELF, send_group)
-    loop(N_Z, N_GRP, send_group)
+    loop(Y_LINE, N_GRP, send_group)
     loop(0, N_BLK - 1, send_loop)
     push_v[SELF] = message(TILES + g)
     push_v[N_FAR - 1] = message(TILES + N_GRP + b)
@@ -299,14 +300,13 @@
 
     loop(0, N_BLK - 1, lambda i: loop_copy(i, push_v, send2_sem, recv2_sem).wait_recv())
     loop(0, LOOP_PAIRS, lambda p: deliver(N_GRP + p * PAIR, lambda q: lt_s[b, loop_at(p * PAIR + q, -1)]))
-    loop(Y_LINE, N_GRP, pushed_group)
+    loop(N_Z // PAIR, GROUP_PAIRS - 2, deliver_group)
+    loop(Y_LINE - 1, N_GRP, pushed_group)
+    deliver_pair(GROUP_PAIRS - 2)
     deliver_pair(GROUP_PAIRS - 1)
     loop(0, SELF // PAIR, deliver_group)
     pushed_group(SELF - 1)
     deliver_pair(SELF // PAIR)
-    loop(N_Z // PAIR, GROUP_PAIRS - 2, deliver_group)
-    pushed_group(Y_LINE - 1)
-    deliver_pair(GROUP_PAIRS - 2)
 
     def sent_group(i):
         group_copy(i, push_v, send2_sem, recv2_sem).wait_send()

time: 114 us -> 113 us (level)
    pallas_call x1, Pallas kernels: 111 us -> 110 us  [body(): pl.pallas_call(kernel, out_shape=[pltpu.VMEM(blocks, f32)] * 2, in_specs=...]
where the time goes in v4:
time: 113 us; the launch traced here: 112 us
  Pallas kernels  112 us (99%)
    pallas_call x1, Pallas kernels, body(): pl.pallas_call(kernel, out_shape=[pltpu.VMEM(blocks, f32)] * 2, in_specs=...  110 us

profile of v4, /device:TPU:1, one launch (start us, length us, event | category | flops | bytes accessed | tf_op | source)
XLA Modules:
  0.0 112.4 jit_solution(8522489541772035932)
XLA Ops:
  0.6 110.1 %shard_map.95 = (f32[12,128,256]{2,1,0:T(8,128)S(1)}, f32[12,128,256]{2,1,0:T(8,128)S(1)}) custom-call(f32[12,128,256]{2,1,0:T(8,128)} %bitcast.9, bf16[12,128,256]{2,1,0:T(8,128)(2,1)} %bitcast.10, bf16[12,128,256]{2,1,0:T(8,128)(2,1)} %bitcast.11, bf16[256,256]{1,0:T(8,128)(2,1)} %w_h.1, s32[12,16]{1,0:T(8,128)} %ids_h.1, bf16[192,128,128]{2,1,0:T(8,128)(2,1)} %bitcast.8, ...), custom_call_target="tpu_custom_call" | custom-call | tf_op jit(solution)/shard_map/pallas_call | solution.py:333
  110.8 1.7 %shard_map.96 = (f32[12,128,256]{2,1,0:T(8,128)}, f32[12,128,256]{2,1,0:T(8,128)}) custom-call(f32[12,128,256]{2,1,0:T(8,128)S(1)} %get-tuple-element.6.out_v, f32[12,128,256]{2,1,0:T(8,128)S(1)} %get-tuple-element.7.box_v), custom_call_target="tpu_custom_call" | custom-call | tf_op jit(solution)/shard_map/pallas_call | solution.py:380

commit v5 on v4

--- a/solution.py
+++ b/solution.py
@@ -15,6 +15,7 @@
 N_FAR = N_GRP + N_BLK
 SELF = N_Z - 1
 Y_LINE = N_GRP - (N_Y - 1)
+Z_FAR = 3
 PAIR = 2
 OWN_PAIRS, LOOP_PAIRS, GROUP_PAIRS = TILES // PAIR, N_BLK // PAIR, N_GRP // PAIR
 BAND = 6
@@ -123,11 +124,12 @@
         pl.semaphore_signal(line_sem, inc=1, device_id={"grp": group_at(i, 1)}, device_id_type=MESH)
 
     loop(Y_LINE, N_GRP, greet_line)
-    loop(0, SELF, pull_group)
+    loop(0, Z_FAR, pull_group)
     loop(Y_LINE, N_GRP, pull_group)
     loop(0, N_BLK - 1, lambda i: loop_copy(i, pull_v, send_sem, recv_sem).start())
     pl.semaphore_wait(line_sem, N_Y - 1)
     loop(N_Z, Y_LINE, pull_group)
+    loop(Z_FAR, SELF, pull_group)
 
     fetch_ids.wait()
     ids = ids_v[...]
@@ -229,14 +231,16 @@
 
     loop(Y_LINE, N_GRP, pulled_group)
     gather(GROUP_PAIRS - 1, pull_v, N_GRP - PAIR)
-    gather_group(0)
-    loop(SELF - 3, SELF, pulled_group)
-    gather(SELF // PAIR - 1, pull_v, SELF - 3, 2)
     loop(2, GROUP_PAIRS // 2 - 1, gather_group)
     pulled_group(Y_LINE - 1)
+    gather(GROUP_PAIRS - 2, pull_v, Y_LINE - 1)
+    gather_group(0)
+    loop(2 * PAIR, SELF - 1, pulled_group)
+    gather(2, pull_v, 2 * PAIR)
+    pulled_group(SELF - 1)
 
     def layer(m):
-        gathered = gath_v[pl.ds(m * BAND, BAND)] + product_of(GROUP_PAIRS - 2, pull_v, Y_LINE - 1, m)
+        gathered = gath_v[pl.ds(m * BAND, BAND)] + product_of(SELF // PAIR, pull_v, SELF - 1, m)
         start = init_v[pl.ds(m * BAND, BAND)].astype(f32)
         mixed = ((1.0 - teleport) * gathered + teleport * start).astype(bf16)
         mixed = mixed.reshape(BAND * EDGE, HIDDEN)

time: 113 us -> 111 us (0.982)
  Pallas kernels: 112 us -> 110 us
    pallas_call x1, Pallas kernels: 110 us -> 108 us  [body(): pl.pallas_call(kernel, out_shape=[pltpu.VMEM(blocks, f32)] * 2, in_specs=...]
where the time goes in v5:
time: 111 us
  Pallas kernels  110 us (99%)
    pallas_call x1, Pallas kernels, body(): pl.pallas_call(kernel, out_shape=[pltpu.VMEM(blocks, f32)] * 2, in_specs=...  108 us

profile of v5, /device:TPU:1, one launch (start us, length us, event | category | flops | bytes accessed | tf_op | source)
XLA Modules:
  0.0 110.6 jit_solution(14177102434183835891)
XLA Ops:
  0.6 108.3 %shard_map.95 = (f32[12,128,256]{2,1,0:T(8,128)S(1)}, f32[12,128,256]{2,1,0:T(8,128)S(1)}) custom-call(f32[12,128,256]{2,1,0:T(8,128)} %bitcast.9, bf16[12,128,256]{2,1,0:T(8,128)(2,1)} %bitcast.10, bf16[12,128,256]{2,1,0:T(8,128)(2,1)} %bitcast.11, bf16[256,256]{1,0:T(8,128)(2,1)} %w_h.1, s32[12,16]{1,0:T(8,128)} %ids_h.1, bf16[192,128,128]{2,1,0:T(8,128)(2,1)} %bitcast.8, ...), custom_call_target="tpu_custom_call" | custom-call | tf_op jit(solution)/shard_map/pallas_call | solution.py:337
  108.9 1.7 %shard_map.96 = (f32[12,128,256]{2,1,0:T(8,128)}, f32[12,128,256]{2,1,0:T(8,128)}) custom-call(f32[12,128,256]{2,1,0:T(8,128)S(1)} %get-tuple-element.6.out_v, f32[12,128,256]{2,1,0:T(8,128)S(1)} %get-tuple-element.7.box_v), custom_call_target="tpu_custom_call" | custom-call | tf_op jit(solution)/shard_map/pallas_call | solution.py:384
